TPU v7x, 32 devices: a whole 2x2x4 slice. The times are simulated.
32 devices in a mesh: tensor: 4 (over y, x), seq: 8 (over z, core).
Axes of the slice: x: 2, y: 2, z: 4, core: 2. Of those that a mesh axis runs over, the one named last changes fastest.
Arguments:
- key_states: bfloat16 [8, 2, 4096, 1024], P(None, None, 'seq', 'tensor'), may hold values from -6 to 6
- value_states: bfloat16 [8, 2, 4096, 1024], P(None, None, 'seq', 'tensor'), may hold values from -6 to 6
- bin_index: int32 [8, 8, 4096], P(None, 'tensor', 'seq'), may hold values from 0 to 4095
- retain_count: int32 [8], replicated, may hold values from 1 to 4096
Outputs:
- histogram: float32 [8, 8, 2, 4096], P(None, 'tensor', None, 'seq')
- threshold: int32 [8], replicated
All inputs are finite; a program needn't handle non-finite values.
Results may differ from a plain program's by a relative error of at most 0.0029.
Values sent between devices are 32-bit elements; how exact they have to be, the bound alone decides.
A program may use at most 64 MiB of HBM per device.

v0:
```python
import functools

import jax
import jax.numpy as jnp
from jax import lax
from jax.experimental import pallas as pl
from jax.experimental.pallas import tpu as pltpu
from jax.sharding import PartitionSpec as P

BINS = 4096
MESH = pl.DeviceIdType.MESH
NT = (((1,), (1,)), ((), ()))
F32 = jnp.float32
BF16 = jnp.bfloat16


def iota(shape, dim):
    return lax.broadcasted_iota(jnp.int32, shape, dim)


def each(lo, hi, body):
    if hi - lo <= 8:
        for k in range(lo, hi):
            body(k)
    else:

        @pl.loop(lo, hi)
        def _(k):
            body(k)


def exact_dot(a, b):
    return jnp.dot(a, b, precision=lax.Precision.HIGHEST, preferred_element_type=F32)


def kernel(
    n, nt, key_hbm, value_hbm, bins, retain, out, threshold,
    kbuf, vbuf, lo_hot, stage_c, recv_c, mine_t, recv_t, all_x, stage_h, recv_h,
    in_sem, cs, cr, ts, tr, gs, gr, hs, hr,
):
    pairs, heads, toks = bins.shape
    width = kbuf.shape[3] // heads
    lanes = stage_c.shape[2]
    per = stage_c.shape[1] // pairs
    his = n * per
    me = lax.axis_index("seq")
    my_t = lax.axis_index("tensor")

    def loads(p):
        return (
            pltpu.make_async_copy(key_hbm.at[p], kbuf.at[p], in_sem.at[0, p]),
            pltpu.make_async_copy(value_hbm.at[p], vbuf.at[p], in_sem.at[1, p]),
        )

    for p in range(pairs):
        for c in loads(p):
            c.start()

    barrier = pltpu.get_barrier_semaphore()

    def greet(k):
        pl.semaphore_signal(barrier, inc=1, device_id={"seq": lax.rem(me + k, n)}, device_id_type=MESH)

    def greet_t(k):
        pl.semaphore_signal(barrier, inc=1, device_id={"tensor": lax.rem(my_t + k, nt)}, device_id_type=MESH)

    each(1, n, greet)
    each(1, nt, greet_t)

    shift = lanes.bit_length() - 1
    for p in range(pairs):
        count = jnp.zeros((his, lanes), F32)
        for h in range(heads):
            row = bins[p, pl.ds(h, 1), :]
            low = row & (lanes - 1)
            high = row >> shift
            lo_mat = jnp.where(iota((lanes, toks), 0) == low, 1.0, 0.0).astype(BF16)
            lo_hot[p, h] = lo_mat
            hi_mat = jnp.where(iota((his, toks), 0) == high, 1.0, 0.0).astype(BF16)
            count += lax.dot_general(hi_mat, lo_mat, NT, preferred_element_type=F32)
        for o in range(n):
            stage_c[o, pl.ds(p * per, per), :] = count[o * per:(o + 1) * per, :]

    pl.semaphore_wait(barrier, n - 1 + nt - 1)

    def copy_c(k):
        peer = lax.rem(me + k, n)
        return pltpu.make_async_remote_copy(
            src_ref=stage_c.at[peer], dst_ref=recv_c.at[k], send_sem=cs.at[k], recv_sem=cr.at[k],
            device_id={"seq": peer}, device_id_type=MESH)

    def copy_t(k):
        return pltpu.make_async_remote_copy(
            src_ref=mine_t, dst_ref=recv_t.at[k], send_sem=ts.at[k], recv_sem=tr.at[k],
            device_id={"tensor": lax.rem(my_t + k, nt)}, device_id_type=MESH)

    def copy_g(k):
        return pltpu.make_async_remote_copy(
            src_ref=all_x.at[me], dst_ref=all_x.at[me], send_sem=gs.at[k], recv_sem=gr.at[k],
            device_id={"seq": lax.rem(me + k, n)}, device_id_type=MESH)

    def copy_h(k, p):
        peer = lax.rem(me + k, n)
        return pltpu.make_async_remote_copy(
            src_ref=stage_h.at[peer, p], dst_ref=recv_h.at[k, p], send_sem=hs.at[k], recv_sem=hr.at[k],
            device_id={"seq": peer}, device_id_type=MESH)

    def copy_h_all(k):
        peer = lax.rem(me + k, n)
        return pltpu.make_async_remote_copy(
            src_ref=stage_h.at[peer], dst_ref=recv_h.at[k], send_sem=hs.at[k], recv_sem=hr.at[k],
            device_id={"seq": peer}, device_id_type=MESH)

    each(1, n, lambda k: copy_c(k).start())

    blk = 128
    eye = iota((blk, blk), 0) == iota((blk, blk), 1)

    def diag(g):
        return jnp.sum(jnp.where(eye, g, 0.0), axis=0, keepdims=True)

    def cosine(buf, p, h):
        parts = []
        for t in range(0, toks, blk):
            a = buf[p, 0, t:t + blk, h * width:(h + 1) * width]
            b = buf[p, 1, t:t + blk, h * width:(h + 1) * width]
            g = lax.dot_general(a, jnp.concatenate([a, b], axis=0), NT, preferred_element_type=F32)
            bb = diag(lax.dot_general(b, b, NT, preferred_element_type=F32))
            aa = diag(g[:, :blk])
            ab = diag(g[:, blk:])
            parts.append(ab / jnp.sqrt((aa + 1.0) * (bb + 1.0)))
        return jnp.concatenate(parts, axis=1)

    odd = (iota((2 * his, toks), 0) & 1) == 1
    hi_of = iota((2 * his, toks), 0) >> 1

    def step(p):
        for c in loads(p):
            c.wait()
        for h in range(heads):
            kc = cosine(kbuf, p, h)
            vc = cosine(vbuf, p, h)
            high = bins[p, pl.ds(h, 1), :] >> shift
            left = jnp.where(hi_of == high, jnp.where(odd, vc, kc), 0.0).astype(BF16)
            res = lax.dot_general(left, lo_hot[p, h], NT, preferred_element_type=F32)
            for o in range(n):
                stage_h[o, p, pl.ds(h * per * 2, per * 2), :] = res[o * per * 2:(o + 1) * per * 2, :]

    def send_h(p):
        each(1, n, lambda k: copy_h(k, p).start())

    third = pairs // 3

    @pl.loop(0, pairs)
    def _(p):
        step(p)
        @pl.when(p >= 1)
        def _():
            send_h(p - 1)

        @pl.when(p == third)
        def _():
            each(1, n, lambda k: copy_c(k).wait_recv())
            mine_t[...] = stage_c[me] + jnp.sum(recv_c[1:n], axis=0)
            each(1, nt, lambda k: copy_t(k).start())

        @pl.when(p == 2 * third)
        def _():
            each(1, nt, lambda k: copy_t(k).wait_recv())
            all_x[me] = mine_t[...] + jnp.sum(recv_t[1:nt], axis=0)
            each(1, n, lambda k: copy_g(k).start())

    send_h(pairs - 1)

    def wait_g(k):
        src = lax.rem(me + n - k, n)
        pltpu.make_async_remote_copy(
            src_ref=all_x.at[src], dst_ref=all_x.at[src], send_sem=gs.at[k], recv_sem=gr.at[k],
            device_id={"seq": lax.rem(me + k, n)}, device_id_type=MESH).wait_recv()

    each(1, n, wait_g)
    rows = pairs * per
    upper = jnp.where(iota((lanes, lanes), 0) <= iota((lanes, lanes), 1), 1.0, 0.0)
    r0, r1 = iota((rows, rows), 0), iota((rows, rows), 1)
    earlier = r1 // per <= r0 // per
    same = jnp.where(earlier & (r1 % per == r0 % per), 1.0, 0.0)
    before = jnp.where(earlier & (r1 % per < r0 % per), 1.0, 0.0)
    whole = jnp.where(earlier, 1.0, 0.0)
    row_pair = iota((rows, lanes), 0) // per
    goal = jnp.zeros((rows, lanes), F32)
    for p in range(pairs):
        goal = jnp.where(row_pair == p, retain[p].astype(F32), goal)

    def scan(r, carry):
        off, cnt = carry
        x = all_x[r]
        xu = exact_dot(x, upper)
        tot = jnp.broadcast_to(jnp.sum(x, axis=1, keepdims=True), (rows, lanes))
        cum = exact_dot(same, xu) + exact_dot(before, tot) + off
        cnt = cnt + jnp.where(cum < goal, 1.0, 0.0)
        return off + exact_dot(whole, tot), cnt

    zero = jnp.zeros((rows, lanes), F32)
    _, cnt = lax.fori_loop(0, n, scan, (zero, zero), unroll=n <= 8)
    for p in range(pairs):
        threshold[p] = jnp.sum(cnt[p * per:(p + 1) * per, :]).astype(jnp.int32)

    each(1, n, lambda k: copy_h_all(k).wait_recv())
    for p in range(pairs):
        acc = stage_h[me, p]
        acc = acc + jnp.sum(recv_h[1:n, p], axis=0)
        for h in range(heads):
            for j in range(per):
                at = (h * per + j) * 2
                out[p, h, :, j * lanes:(j + 1) * lanes] = acc[at:at + 2, :]

    each(1, n, lambda k: copy_c(k).wait_send())
    each(1, nt, lambda k: copy_t(k).wait_send())
    each(1, n, lambda k: copy_g(k).wait_send())
    each(1, n, lambda k: copy_h_all(k).wait_send())


def solution(mesh):
    n, nt = mesh.shape["seq"], mesh.shape["tensor"]

    def per_device(key_states, value_states, bin_index, retain_count):
        pairs, heads, toks = bin_index.shape
        span = BINS // n
        lanes = min(128, span)
        per = span // lanes
        rows = pairs * per
        vmem = pltpu.VMEM
        dma = pltpu.SemaphoreType.DMA
        return pl.pallas_call(
            functools.partial(kernel, n, nt),
            out_shape=(
                jax.ShapeDtypeStruct((pairs, heads, 2, span), F32),
                jax.ShapeDtypeStruct((pairs,), jnp.int32),
            ),
            in_specs=[
                pl.BlockSpec(memory_space=pl.ANY),
                pl.BlockSpec(memory_space=pl.ANY),
                pl.BlockSpec(memory_space=vmem),
                pl.BlockSpec(memory_space=pltpu.SMEM),
            ],
            out_specs=(pl.BlockSpec(memory_space=vmem), pl.BlockSpec(memory_space=pltpu.SMEM)),
            scratch_shapes=[
                vmem(key_states.shape, BF16),
                vmem(value_states.shape, BF16),
                vmem((pairs, heads, lanes, toks), BF16),
                vmem((n, rows, lanes), F32),
                vmem((n, rows, lanes), F32),
                vmem((rows, lanes), F32),
                vmem((nt, rows, lanes), F32),
                vmem((n, rows, lanes), F32),
                vmem((n, pairs, heads * per * 2, lanes), F32),
                vmem((n, pairs, heads * per * 2, lanes), F32),
                dma((2, pairs)),
                dma((n,)), dma((n,)), dma((nt,)), dma((nt,)),
                dma((n,)), dma((n,)), dma((n,)), dma((n,)),
            ],
            compiler_params=pltpu.CompilerParams(collective_id=0, has_side_effects=True),
        )(key_states, value_states, bin_index, retain_count)

    in_specs = (
        P(None, None, "seq", "tensor"),
        P(None, None, "seq", "tensor"),
        P(None, "tensor", "seq"),
        P(),
    )
    out_specs = (P(None, "tensor", None, "seq"), P())
    return jax.shard_map(
        per_device, mesh=mesh, in_specs=in_specs, out_specs=out_specs, check_vma=False
    )
```

profile of v0, /device:TPU:0, one launch (start us, length us, event | category | flops | bytes accessed | tf_op | source)
XLA Modules:
  0.0 29.5 jit_solution(2569824090114654319)
XLA Ops:
  0.6 26.3 %shard_map.59 = (f32[8,2,2,512]{3,2,1,0:T(2,128)}, s32[8]{0:T(128)}) custom-call(bf16[8,2,512,256]{3,2,1,0:T(8,128)(2,1)} %key_hbm.1, bf16[8,2,512,256]{3,2,1,0:T(8,128)(2,1)} %value_hbm.1, s32[8,2,512]{2,1,0:T(2,128)} %bins.1, s32[8]{0:T(128)} %retain.1), custom_call_target="tpu_custom_call" | custom-call | tf_op jit(solution)/shard_map/pallas_call | solution.py:234
  26.9 1.5 %copy.8 = f32[8,2,2,512]{3,2,1,0:T(2,128)} copy(f32[8,2,2,512]{3,2,1,0:T(2,128)} %get-tuple-element.4) | data formatting | bytes 131072
  28.4 1.1 %copy.9 = s32[8]{0:T(128)} copy(s32[8]{0:T(128)} %get-tuple-element.5) | data formatting | bytes 64
where the time goes:
time: 29.8 us; the launch traced here: 29.5 us
  Pallas kernels  26.3 us (88%)
  local copies, waits for them, and re-layouts  2.59 us (9%)
  between operations  0.64 us (2%)
    pallas_call x1, Pallas kernels, per_device(): pl.pallas_call(functools.partial(kernel, n, nt), out_shape=(jax.ShapeDtyp...  26.3 us
    unnamed x2, local copies, waits for them, and re-layouts  2.59 us

commit v1 on v0

v1 whole, which is shorter than its diff:
```python
import functools

import jax
import jax.numpy as jnp
from jax import lax
from jax.experimental import pallas as pl
from jax.experimental.pallas import tpu as pltpu
from jax.sharding import PartitionSpec as P

BINS = 4096
MESH = pl.DeviceIdType.MESH
NT = (((1,), (1,)), ((), ()))
F32 = jnp.float32
BF16 = jnp.bfloat16


def iota(shape, dim):
    return lax.broadcasted_iota(jnp.int32, shape, dim)


def each(lo, hi, body):
    if hi - lo <= 8:
        for k in range(lo, hi):
            body(k)
    else:

        @pl.loop(lo, hi)
        def _(k):
            body(k)


def exact_dot(a, b):
    return jnp.dot(a, b, precision=lax.Precision.HIGHEST, preferred_element_type=F32)


def kernel(
    n, nt, key_hbm, value_hbm, bins, retain, out, threshold,
    kbuf, vbuf, lo_hot, stage_c, recv_c, mine_t, recv_t, all_x, stage_h, recv_d, comb, recv_h,
    in_sem, cs, cr, ts, tr, gs, gr, ds, dr, hs, hr,
):
    pairs, heads, toks = bins.shape
    width = kbuf.shape[3] // heads
    lanes = stage_c.shape[2]
    his = BINS // lanes
    per = his // n
    group, chips = 2 * nt, n // 2
    per_c = his // group
    me = lax.axis_index("seq")
    my_t = lax.axis_index("tensor")
    chip, core = me // 2, me % 2
    spot = my_t * 2 + core

    def in_plane(k):
        g = lax.rem(spot + k, group)
        return g, {"seq": chip * 2 + g % 2, "tensor": g // 2}

    def in_line(k):
        z = lax.rem(chip + k, chips)
        return z, {"seq": z * 2 + core}

    def loads(p):
        return (
            pltpu.make_async_copy(key_hbm.at[p], kbuf.at[p], in_sem.at[0, p]),
            pltpu.make_async_copy(value_hbm.at[p], vbuf.at[p], in_sem.at[1, p]),
        )

    for p in range(pairs):
        for c in loads(p):
            c.start()

    barrier = pltpu.get_barrier_semaphore()

    def greet(k):
        pl.semaphore_signal(barrier, inc=1, device_id=in_plane(k)[1], device_id_type=MESH)

    def greet_line(k):
        pl.semaphore_signal(barrier, inc=1, device_id=in_line(k)[1], device_id_type=MESH)

    each(1, group, greet)
    each(1, chips, greet_line)

    shift = lanes.bit_length() - 1
    for p in range(pairs):
        count = jnp.zeros((his, lanes), F32)
        for h in range(heads):
            row = bins[p, pl.ds(h, 1), :]
            low = row & (lanes - 1)
            high = row >> shift
            lo_mat = jnp.where(iota((lanes, toks), 0) == low, 1.0, 0.0).astype(BF16)
            lo_hot[p, h] = lo_mat
            hi_mat = jnp.where(iota((his, toks), 0) == high, 1.0, 0.0).astype(BF16)
            count += lax.dot_general(hi_mat, lo_mat, NT, preferred_element_type=F32)
        for o in range(group):
            stage_c[o, pl.ds(p * per_c, per_c), :] = count[o * per_c:(o + 1) * per_c, :]

    pl.semaphore_wait(barrier, group - 1 + chips - 1)

    def copy_c(k):
        g, device = in_plane(k)
        return pltpu.make_async_remote_copy(
            src_ref=stage_c.at[g], dst_ref=recv_c.at[k], send_sem=cs.at[k], recv_sem=cr.at[k],
            device_id=device, device_id_type=MESH)

    def copy_t(k):
        return pltpu.make_async_remote_copy(
            src_ref=mine_t, dst_ref=recv_t.at[k], send_sem=ts.at[k], recv_sem=tr.at[k],
            device_id=in_line(k)[1], device_id_type=MESH)

    def copy_g(k, slot):
        return pltpu.make_async_remote_copy(
            src_ref=all_x.at[slot], dst_ref=all_x.at[slot], send_sem=gs.at[k], recv_sem=gr.at[k],
            device_id=in_plane(k)[1], device_id_type=MESH)

    def copy_d(p):
        return pltpu.make_async_remote_copy(
            src_ref=stage_h.at[p, 1 - core], dst_ref=recv_d.at[p], send_sem=ds.at[p], recv_sem=dr.at[p],
            device_id={"seq": chip * 2 + 1 - core}, device_id_type=MESH)

    def copy_h(k, p):
        z, device = in_line(k)
        return pltpu.make_async_remote_copy(
            src_ref=comb.at[z, p], dst_ref=recv_h.at[k, p], send_sem=hs.at[k], recv_sem=hr.at[k],
            device_id=device, device_id_type=MESH)

    def copy_h_all(k):
        z, device = in_line(k)
        return pltpu.make_async_remote_copy(
            src_ref=comb.at[z], dst_ref=recv_h.at[k], send_sem=hs.at[k], recv_sem=hr.at[k],
            device_id=device, device_id_type=MESH)

    each(1, group, lambda k: copy_c(k).start())

    blk = 128
    eye = iota((blk, blk), 0) == iota((blk, blk), 1)

    def diag(g):
        return jnp.sum(jnp.where(eye, g, 0.0), axis=0, keepdims=True)

    def cosine(buf, p, h):
        parts = []
        for t in range(0, toks, blk):
            a = buf[p, 0, t:t + blk, h * width:(h + 1) * width]
            b = buf[p, 1, t:t + blk, h * width:(h + 1) * width]
            g = lax.dot_general(a, jnp.concatenate([a, b], axis=0), NT, preferred_element_type=F32)
            bb = diag(lax.dot_general(b, b, NT, preferred_element_type=F32))
            aa = diag(g[:, :blk])
            ab = diag(g[:, blk:])
            parts.append(ab / jnp.sqrt((aa + 1.0) * (bb + 1.0)))
        return jnp.concatenate(parts, axis=1)

    odd = (iota((2 * his, toks), 0) & 1) == 1
    hi_of = iota((2 * his, toks), 0) >> 1

    def step(p):
        for c in loads(p):
            c.wait()
        for h in range(heads):
            kc = cosine(kbuf, p, h)
            vc = cosine(vbuf, p, h)
            high = bins[p, pl.ds(h, 1), :] >> shift
            left = jnp.where(hi_of == high, jnp.where(odd, vc, kc), 0.0).astype(BF16)
            res = lax.dot_general(left, lo_hot[p, h], NT, preferred_element_type=F32)
            for o in range(n):
                stage_h[p, o % 2, o // 2, pl.ds(h * per * 2, per * 2), :] = res[o * per * 2:(o + 1) * per * 2, :]

    def merge(p):
        copy_d(p).wait_recv()
        comb[:, p] = stage_h[p, core] + recv_d[p]

    def send_h(p):
        each(1, chips, lambda k: copy_h(k, p).start())

    third = pairs // 3

    @pl.loop(0, pairs)
    def _(p):
        step(p)

        @pl.when(p >= 1)
        def _():
            merge(p - 1)

        copy_d(p).start()

        @pl.when(p >= 1)
        def _():
            send_h(p - 1)

        @pl.when(p == third)
        def _():
            each(1, group, lambda k: copy_c(k).wait_recv())
            mine_t[...] = stage_c[spot] + jnp.sum(recv_c[1:group], axis=0)
            each(1, chips, lambda k: copy_t(k).start())

        @pl.when(p == 2 * third + 1)
        def _():
            each(1, chips, lambda k: copy_t(k).wait_recv())
            all_x[spot] = mine_t[...] + jnp.sum(recv_t[1:chips], axis=0)
            each(1, group, lambda k: copy_g(k, spot).start())

    merge(pairs - 1)
    send_h(pairs - 1)

    each(1, group, lambda k: copy_g(k, lax.rem(spot + group - k, group)).wait_recv())
    rows = pairs * per_c
    upper = jnp.where(iota((lanes, lanes), 0) <= iota((lanes, lanes), 1), 1.0, 0.0)
    r0, r1 = iota((rows, rows), 0), iota((rows, rows), 1)
    earlier = r1 // per_c <= r0 // per_c
    same = jnp.where(earlier & (r1 % per_c == r0 % per_c), 1.0, 0.0)
    before = jnp.where(earlier & (r1 % per_c < r0 % per_c), 1.0, 0.0)
    whole = jnp.where(earlier, 1.0, 0.0)
    row_pair = iota((rows, lanes), 0) // per_c
    goal = jnp.zeros((rows, lanes), F32)
    for p in range(pairs):
        goal = jnp.where(row_pair == p, retain[p].astype(F32), goal)

    def scan(r, carry):
        off, cnt = carry
        x = all_x[r]
        xu = exact_dot(x, upper)
        tot = jnp.broadcast_to(jnp.sum(x, axis=1, keepdims=True), (rows, lanes))
        cum = exact_dot(same, xu) + exact_dot(before, tot) + off
        cnt = cnt + jnp.where(cum < goal, 1.0, 0.0)
        return off + exact_dot(whole, tot), cnt

    zero = jnp.zeros((rows, lanes), F32)
    _, cnt = lax.fori_loop(0, group, scan, (zero, zero), unroll=group <= 8)
    for p in range(pairs):
        threshold[p] = jnp.sum(cnt[p * per_c:(p + 1) * per_c, :]).astype(jnp.int32)

    each(1, chips, lambda k: copy_h_all(k).wait_recv())
    for p in range(pairs):
        acc = comb[chip, p] + jnp.sum(recv_h[1:chips, p], axis=0)
        for h in range(heads):
            for j in range(per):
                at = (h * per + j) * 2
                out[p, h, :, j * lanes:(j + 1) * lanes] = acc[at:at + 2, :]

    each(1, group, lambda k: copy_c(k).wait_send())
    each(1, chips, lambda k: copy_t(k).wait_send())
    each(1, group, lambda k: copy_g(k, spot).wait_send())
    each(0, pairs, lambda p: copy_d(p).wait_send())
    each(1, chips, lambda k: copy_h_all(k).wait_send())


def solution(mesh):
    n, nt = mesh.shape["seq"], mesh.shape["tensor"]

    def per_device(key_states, value_states, bin_index, retain_count):
        pairs, heads, toks = bin_index.shape
        span = BINS // n
        lanes = min(128, span)
        per = span // lanes
        group, chips = 2 * nt, n // 2
        rows = pairs * BINS // lanes // group
        block = (heads * per * 2, lanes)
        vmem = pltpu.VMEM
        dma = pltpu.SemaphoreType.DMA
        return pl.pallas_call(
            functools.partial(kernel, n, nt),
            out_shape=(
                jax.ShapeDtypeStruct((pairs, heads, 2, span), F32),
                jax.ShapeDtypeStruct((pairs,), jnp.int32),
            ),
            in_specs=[
                pl.BlockSpec(memory_space=pl.ANY),
                pl.BlockSpec(memory_space=pl.ANY),
                pl.BlockSpec(memory_space=vmem),
                pl.BlockSpec(memory_space=pltpu.SMEM),
            ],
            out_specs=(pl.BlockSpec(memory_space=vmem), pl.BlockSpec(memory_space=pltpu.SMEM)),
            scratch_shapes=[
                vmem(key_states.shape, BF16),
                vmem(value_states.shape, BF16),
                vmem((pairs, heads, lanes, toks), BF16),
                vmem((group, rows, lanes), F32),
                vmem((group, rows, lanes), F32),
                vmem((rows, lanes), F32),
                vmem((chips, rows, lanes), F32),
                vmem((group, rows, lanes), F32),
                vmem((pairs, 2, chips) + block, F32),
                vmem((pairs, chips) + block, F32),
                vmem((chips, pairs) + block, F32),
                vmem((chips, pairs) + block, F32),
                dma((2, pairs)),
                dma((group,)), dma((group,)), dma((chips,)), dma((chips,)),
                dma((group,)), dma((group,)), dma((pairs,)), dma((pairs,)),
                dma((chips,)), dma((chips,)),
            ],
            compiler_params=pltpu.CompilerParams(collective_id=0, has_side_effects=True),
        )(key_states, value_states, bin_index, retain_count)

    in_specs = (
        P(None, None, "seq", "tensor"),
        P(None, None, "seq", "tensor"),
        P(None, "tensor", "seq"),
        P(),
    )
    out_specs = (P(None, "tensor", None, "seq"), P())
    return jax.shard_map(
        per_device, mesh=mesh, in_specs=in_specs, out_specs=out_specs, check_vma=False
    )
```

time: 29.8 us -> 25.7 us (0.86)
  Pallas kernels: 26.3 us -> 22.2 us
    pallas_call x1, Pallas kernels: 26.3 us -> 22.2 us  [per_device(): pl.pallas_call(functools.partial(kernel, n, nt), out_shape=(jax.ShapeDtyp...]
where the time goes in v1:
time: 25.7 us; the launch traced here: 25.4 us
  Pallas kernels  22.2 us (86%)
  local copies, waits for them, and re-layouts  2.59 us (10%)
  between operations  0.64 us (2%)
    pallas_call x1, Pallas kernels, per_device(): pl.pallas_call(functools.partial(kernel, n, nt), out_shape=(jax.ShapeDtyp...  22.2 us
    unnamed x2, local copies, waits for them, and re-layouts  2.59 us

profile of v1, /device:TPU:0, one launch (start us, length us, event | category | flops | bytes accessed | tf_op | source)
XLA Modules:
  0.0 25.4 jit_solution(1382415646421240865)
XLA Ops:
  0.6 22.2 %shard_map.59 = (f32[8,2,2,512]{3,2,1,0:T(2,128)}, s32[8]{0:T(128)}) custom-call(bf16[8,2,512,256]{3,2,1,0:T(8,128)(2,1)} %key_hbm.1, bf16[8,2,512,256]{3,2,1,0:T(8,128)(2,1)} %value_hbm.1, s32[8,2,512]{2,1,0:T(2,128)} %bins.1, s32[8]{0:T(128)} %retain.1), custom_call_target="tpu_custom_call" | custom-call | tf_op jit(solution)/shard_map/pallas_call | solution.py:259
  22.8 1.5 %copy.8 = f32[8,2,2,512]{3,2,1,0:T(2,128)} copy(f32[8,2,2,512]{3,2,1,0:T(2,128)} %get-tuple-element.4) | data formatting | bytes 131072
  24.3 1.1 %copy.9 = s32[8]{0:T(128)} copy(s32[8]{0:T(128)} %get-tuple-element.5) | data formatting | bytes 64
